TPU v7x, 32 devices: a whole 2x2x4 slice. The times are simulated.
32 devices in a mesh: seq: 8 (over y, x, core), ch: 4 (over z).
Axes of the slice: x: 2, y: 2, z: 4, core: 2. Of those that a mesh axis runs over, the one named last changes fastest.
Arguments:
- inputs: bfloat16 [256, 4096], P('ch', 'seq'), may hold values from -6 to 6
- w_value: bfloat16 [256, 256], P(None, 'ch'), may hold values from -0.375 to 0.375
- w_gate: bfloat16 [256, 256], P(None, 'ch'), may hold values from -0.375 to 0.375
- w_out: bfloat16 [256, 256], P('ch'), may hold values from -0.375 to 0.375
- filter_taps: float32 [256, 4096], P('ch', 'seq'), may hold values from -6 to 6
- grad_out: bfloat16 [256, 4096], P('ch', 'seq'), may hold values from -6 to 6
Outputs:
- d_inputs: bfloat16 [256, 4096], P('ch', 'seq')
- d_w_value: float32 [256, 256], P(None, 'ch')
- d_w_gate: float32 [256, 256], P(None, 'ch')
- d_w_out: float32 [256, 256], P('ch')
- d_filter: float32 [256, 4096], P('ch', 'seq')
All inputs are finite; a program needn't handle non-finite values.
Results may differ from a plain program's by a relative error of at most 0.015.
Values may be sent and summed in bfloat16 or wider, within the bound.
A program may use at most 64 MiB of HBM per device.

v0:
```python
import functools
import math

import jax
import jax.numpy as jnp
import numpy as np
from jax import lax
from jax.experimental import pallas as pl
from jax.experimental.pallas import tpu as pltpu
from jax.sharding import PartitionSpec as P

F32 = jnp.float32
BF16 = jnp.bfloat16
LANES = 128


def dft_tables(strides, lanes, chans):
    length = 2 * strides * lanes
    n1 = np.arange(strides)
    n2 = np.arange(lanes)
    half = np.arange(strides) + 0.5
    first = np.exp(-2j * np.pi * np.outer(half, n1) / (2 * strides))
    eye = np.eye(chans)
    first_re, first_im = np.kron(first.real, eye), np.kron(first.imag, eye)
    ahead = np.concatenate([first_re, first_im], 0)
    twist = np.repeat(np.exp(-2j * np.pi * np.outer(half, n2) / length), chans, axis=0)
    last = np.exp(-2j * np.pi * np.outer(n2, n2) / lanes)
    c, s = last.real, last.imag
    across = np.block([[c, s], [-s, c]])
    low = lambda a: jnp.asarray(a.astype(np.float32)).astype(BF16)
    wide = lambda a: jnp.asarray(a.astype(np.float32))
    return (
        low(ahead),
        low(ahead.T * (2.0 / length)),
        low(across),
        low(across.T),
        wide(np.stack([twist.real, twist.imag])),
    )


def each(count, step):
    if count <= 16:
        for k in range(count):
            step(k)
    else:
        lax.fori_loop(0, count, lambda k, carry: (step(k), carry)[1], 0)


def body(
    groups, rings, scale,
    in_ref, wv_ref, wg_ref, wo_ref, filt_ref, grad_ref, ahead_ref, back_ref, across_ref, return_ref, twist_ref,
    din_ref, dwv_ref, dwg_ref, dwo_ref, dfil_ref,
    full_in, full_grad, got_filt, out_val, got_val, out_dif, got_dif,
    out_mix, got_mix, out_dv, got_dv, out_df, got_df,
    out_din, got_din, out_w, got_w, out_ws, got_ws,
    seq_send, seq_recv, ch_send, ch_recv,
):
    me = lax.axis_index("seq")
    mc = lax.axis_index("ch")
    ch_rows, tokens = in_ref.shape
    chans = ch_rows // groups
    tiles = tokens // LANES
    width = full_in.shape[0] * ch_rows
    barrier = pltpu.get_barrier_semaphore()

    def seq_peer(k):
        return lax.rem(me + k, groups)

    def seq_from(k):
        return lax.rem(me + groups - k, groups)

    def ch_peer(k):
        return lax.rem(mc + k, rings)

    def ch_from(k):
        return lax.rem(mc + rings - k, rings)

    each(groups - 1, lambda k: pl.semaphore_signal(
        barrier, inc=1, device_id={"seq": seq_peer(k + 1)}, device_id_type=pl.DeviceIdType.MESH))
    each(rings - 1, lambda k: pl.semaphore_signal(
        barrier, inc=1, device_id={"ch": ch_peer(k + 1)}, device_id_type=pl.DeviceIdType.MESH))
    pl.semaphore_wait(barrier, groups + rings - 2)

    def seq_copy(stage, src, dst, k, pick):
        return pltpu.make_async_remote_copy(
            src_ref=src.at[seq_peer(k)] if pick else src,
            dst_ref=dst.at[me],
            send_sem=seq_send.at[stage, k],
            recv_sem=seq_recv.at[stage, k],
            device_id={"seq": seq_peer(k)},
            device_id_type=pl.DeviceIdType.MESH,
        )

    def ch_copy(stage, src, dst, k, pick):
        return pltpu.make_async_remote_copy(
            src_ref=src.at[ch_peer(k)] if pick else src,
            dst_ref=dst.at[mc],
            send_sem=ch_send.at[stage, k],
            recv_sem=ch_recv.at[stage, k],
            device_id={"ch": ch_peer(k)},
            device_id_type=pl.DeviceIdType.MESH,
        )

    def seq_start(stage, src, dst, pick=True):
        each(groups - 1, lambda k: seq_copy(stage, src, dst, k + 1, pick).start())

    def seq_wait(stage, src, dst, pick=True):
        each(groups - 1, lambda k: seq_copy(stage, src, dst, k + 1, pick).wait_recv())

    def seq_done(stage, src, dst, pick=True):
        each(groups - 1, lambda k: seq_copy(stage, src, dst, k + 1, pick).wait_send())

    def ch_start(stage, src, dst, pick=False):
        each(rings - 1, lambda k: ch_copy(stage, src, dst, k + 1, pick).start())

    def ch_wait(stage, src, dst, pick=False):
        each(rings - 1, lambda k: ch_copy(stage, src, dst, k + 1, pick).wait_recv())

    def ch_done(stage, src, dst, pick=False):
        each(rings - 1, lambda k: ch_copy(stage, src, dst, k + 1, pick).wait_send())

    ch_start(0, in_ref, full_in)
    ch_start(1, grad_ref, full_grad)
    seq_start(0, filt_ref, got_filt)
    full_in[mc] = in_ref[...]
    full_grad[mc] = grad_ref[...]
    got_filt[me] = filt_ref[me]

    def by_owner(x):
        x = x.reshape(groups, chans, tokens)
        return jnp.concatenate([x[:, :, j * LANES:(j + 1) * LANES] for j in range(tiles)], axis=1)

    def by_token(x):
        x = x.astype(F32)
        x = jnp.concatenate([x[:, j * chans:(j + 1) * chans, :] for j in range(tiles)], axis=2)
        return x.reshape(ch_rows, tokens)

    def stacked(ref):
        return jnp.concatenate([ref[p] for p in range(groups)], axis=0).astype(BF16)

    ahead = ahead_ref[...]
    across = across_ref[...]
    rows = ahead.shape[1]
    tw_re, tw_im = twist_ref[0], twist_ref[1]

    def dot(a, b):
        return jnp.dot(a, b, preferred_element_type=F32)

    def spectrum(x):
        first = dot(ahead, x)
        re, im = first[:rows], first[rows:]
        mid = jnp.concatenate([re * tw_re - im * tw_im, re * tw_im + im * tw_re], axis=1).astype(BF16)
        out = dot(mid, across)
        return out[:, :LANES], out[:, LANES:]

    def signal(re, im):
        mid = dot(jnp.concatenate([re, im], axis=1).astype(BF16), return_ref[...])
        re, im = mid[:, :LANES], mid[:, LANES:]
        tall = jnp.concatenate([re * tw_re + im * tw_im, im * tw_re - re * tw_im], axis=0).astype(BF16)
        return dot(back_ref[...], tall).reshape(groups, tiles * chans, LANES)

    ch_wait(0, in_ref, full_in)
    x_in = full_in[...].reshape(width, tokens)
    over_first = (((0,), (0,)), ((), ()))
    value = lax.dot_general(wv_ref[...], x_in, over_first, preferred_element_type=F32)
    out_val[...] = by_owner(value).astype(BF16)
    seq_start(1, out_val, got_val)
    got_val[me] = out_val[me]
    gate = lax.dot_general(wg_ref[...], x_in, over_first, preferred_element_type=F32)

    ch_wait(1, grad_ref, full_grad)
    x_grad = full_grad[...].reshape(width, tokens)
    d_gated = dot(wo_ref[...], x_grad)
    out_dif[...] = by_owner(d_gated * gate).astype(BF16)
    seq_start(2, out_dif, got_dif)
    got_dif[me] = out_dif[me]

    seq_wait(0, filt_ref, got_filt)
    by_tile = jnp.concatenate(
        [got_filt[p][:, j * LANES:(j + 1) * LANES] for p in range(groups) for j in range(tiles)], axis=0)
    f_re, f_im = spectrum(by_tile.astype(BF16))
    seq_wait(1, out_val, got_val)
    v_re, v_im = spectrum(stacked(got_val))
    out_mix[...] = signal(f_re * v_re - f_im * v_im, f_re * v_im + f_im * v_re).astype(BF16)
    seq_start(3, out_mix, got_mix)
    got_mix[me] = out_mix[me]

    seq_wait(2, out_dif, got_dif)
    g_re, g_im = spectrum(stacked(got_dif))
    out_dv[...] = signal(f_re * g_re + f_im * g_im, f_re * g_im - f_im * g_re).astype(BF16)
    seq_start(4, out_dv, got_dv)
    got_dv[me] = out_dv[me]
    out_df[...] = signal(v_re * g_re + v_im * g_im, v_re * g_im - v_im * g_re).astype(BF16)
    seq_start(5, out_df, got_df)
    got_df[me] = out_df[me]

    over_last = (((1,), (1,)), ((), ()))
    seq_wait(3, out_mix, got_mix)
    mixed = by_token(got_mix[...])
    gated_out = (gate * mixed).astype(BF16)
    d_gate = (d_gated * mixed).astype(BF16)
    from_gate = dot(wg_ref[...], d_gate)
    out_term = lax.dot_general(gated_out, x_grad, over_last, preferred_element_type=F32)

    seq_wait(4, out_dv, got_dv)
    d_value = by_token(got_dv[...]).astype(BF16)
    d_in = dot(wv_ref[...], d_value) + from_gate
    out_din[...] = d_in.reshape(rings, ch_rows, tokens).astype(BF16)
    ch_start(2, out_din, got_din, True)
    pair_term = lax.dot_general(
        x_in, jnp.concatenate([d_value, d_gate], axis=0), over_last, preferred_element_type=F32)
    pair_rows = width // groups
    pair = pair_term.reshape(groups, pair_rows, 2 * ch_rows)
    outs = out_term.reshape(groups, chans, width)
    out_w[...] = jnp.concatenate(
        [pair] + [outs[:, :, j * LANES:(j + 1) * LANES] for j in range(width // LANES)], axis=1).astype(BF16)
    seq_start(6, out_w, got_w)
    got_w[me] = out_w[me]
    got_din[mc] = out_din[mc]

    seq_wait(6, out_w, got_w)
    total = got_w[0].astype(F32)
    for p in range(1, groups):
        total = total + got_w[p].astype(F32)
    out_ws[...] = total.astype(BF16)
    seq_start(7, out_ws, got_ws, False)
    got_ws[me] = out_ws[...]

    seq_wait(5, out_df, got_df)
    dfil_ref[...] = by_token(got_df[...]) * scale

    ch_wait(2, out_din, got_din, True)
    d_sum = got_din[0].astype(F32)
    for p in range(1, rings):
        d_sum = d_sum + got_din[p].astype(F32)
    din_ref[...] = d_sum.astype(BF16)

    seq_wait(7, out_ws, got_ws, False)
    summed = got_ws[...].astype(F32) * scale
    pair = summed[:, :pair_rows, :].reshape(width, 2 * ch_rows)
    dwv_ref[...] = pair[:, :ch_rows]
    dwg_ref[...] = pair[:, ch_rows:]
    dwo_ref[...] = jnp.concatenate(
        [summed[:, pair_rows + j * chans:pair_rows + (j + 1) * chans, :] for j in range(width // LANES)],
        axis=2).reshape(ch_rows, width)

    ch_done(0, in_ref, full_in)
    ch_done(1, grad_ref, full_grad)
    ch_done(2, out_din, got_din, True)
    for stage, src, dst, pick in (
        (0, filt_ref, got_filt, True), (1, out_val, got_val, True), (2, out_dif, got_dif, True),
        (3, out_mix, got_mix, True), (4, out_dv, got_dv, True), (5, out_df, got_df, True),
        (6, out_w, got_w, True), (7, out_ws, got_ws, False),
    ):
        seq_done(stage, src, dst, pick)


def solution(mesh):
    groups, rings = mesh.shape["seq"], mesh.shape["ch"]

    def on_device(inputs, w_value, w_gate, w_out, filter_taps, grad_out):
        ch_rows, tokens = inputs.shape
        width = w_value.shape[0]
        chans, tiles = ch_rows // groups, tokens // LANES
        tables = dft_tables(groups * tiles, LANES, chans)
        scale = 1.0 / math.sqrt(tokens * groups)
        vmem = pl.BlockSpec(memory_space=pltpu.VMEM)
        block = pltpu.VMEM((groups, tiles * chans, LANES), BF16)
        share = width // groups + chans * (width // LANES)
        return pl.pallas_call(
            functools.partial(body, groups, rings, scale),
            out_shape=(
                jax.ShapeDtypeStruct((ch_rows, tokens), BF16),
                jax.ShapeDtypeStruct((width, ch_rows), F32),
                jax.ShapeDtypeStruct((width, ch_rows), F32),
                jax.ShapeDtypeStruct((ch_rows, width), F32),
                jax.ShapeDtypeStruct((ch_rows, tokens), F32),
            ),
            in_specs=[vmem] * 11,
            out_specs=(vmem,) * 5,
            scratch_shapes=[
                pltpu.VMEM((rings, ch_rows, tokens), BF16),
                pltpu.VMEM((rings, ch_rows, tokens), BF16),
                pltpu.VMEM((groups, chans, tokens), F32),
            ] + [block] * 10 + [
                pltpu.VMEM((rings, ch_rows, tokens), BF16),
                pltpu.VMEM((rings, ch_rows, tokens), BF16),
                pltpu.VMEM((groups, share, 2 * ch_rows), BF16),
                pltpu.VMEM((groups, share, 2 * ch_rows), BF16),
                pltpu.VMEM((share, 2 * ch_rows), BF16),
                pltpu.VMEM((groups, share, 2 * ch_rows), BF16),
                pltpu.SemaphoreType.DMA((8, groups)),
                pltpu.SemaphoreType.DMA((8, groups)),
                pltpu.SemaphoreType.DMA((3, rings)),
                pltpu.SemaphoreType.DMA((3, rings)),
            ],
            compiler_params=pltpu.CompilerParams(collective_id=0, has_side_effects=True),
        )(
            inputs, w_value, w_gate, w_out, filter_taps.reshape(groups, chans, tokens), grad_out, *tables,
        )

    return jax.shard_map(
        on_device,
        mesh=mesh,
        in_specs=(P("ch", "seq"), P(None, "ch"), P(None, "ch"), P("ch", None), P("ch", "seq"), P("ch", "seq")),
        out_specs=(P("ch", "seq"), P(None, "ch"), P(None, "ch"), P("ch", None), P("ch", "seq")),
        check_vma=False,
    )
```

profile of v0, /device:TPU:0, one launch (start us, length us, event | category | flops | bytes accessed | tf_op | source)
XLA Modules:
  0.0 43.3 jit_solution(849104317995158839)
XLA Ops:
  0.6 0.0 copy-start.4
  0.6 1.5 %copy.16.wv_ref = bf16[256,64]{1,0:T(8,128)(2,1)} copy(bf16[256,64]{0,1:T(8,128)(2,1)} %param.12) | data formatting | bytes 65536 | tf_op args[1]
  2.1 0.0 copy-done.4
  2.1 0.7 %copy.17.wg_ref = bf16[256,64]{1,0:T(8,128)(2,1)} copy(bf16[256,64]{0,1:T(8,128)(2,1)S(1)} %copy-done.4) | data formatting | bytes 65536 | tf_op args[2]
  2.9 35.9 %shard_map.146 = (bf16[64,512]{1,0:T(8,128)(2,1)}, f32[256,64]{1,0:T(8,128)}, f32[256,64]{1,0:T(8,128)}, f32[64,256]{1,0:T(8,128)}, f32[64,512]{1,0:T(8,128)}) custom-call(bf16[64,512]{1,0:T(8,128)(2,1)} %in_ref.1, bf16[256,64]{1,0:T(8,128)(2,1)} %copy.16.wv_ref, bf16[256,64]{1,0:T(8,128)(2,1)} %copy.17.wg_ref, bf16[64,256]{1,0:T(8,128)(2,1)} %wo_ref.1, ...), custom_call_target="tpu_custom_call" | custom-call | tf_op jit(solution)/shard_map/pallas_call | solution.py:270
  38.8 0.0 copy-start
  38.8 1.7 %copy.18 = f32[256,64]{0,1:T(8,128)} copy(f32[256,64]{1,0:T(8,128)} %get-tuple-element.6) | data formatting | bytes 131072 | tf_op jit(solution)/shard_map/pallas_call | solution.py:270
  40.5 0.0 copy-done
  40.5 0.0 copy-start.3
  40.5 0.0 copy-start.2
  40.5 0.7 %copy.19 = f32[256,64]{0,1:T(8,128)} copy(f32[256,64]{1,0:T(8,128)S(1)} %copy-done) | data formatting | bytes 131072 | tf_op jit(solution)/shard_map/pallas_call | solution.py:270
  41.2 0.1 copy-done.3
  41.3 0.0 copy-start.1
  41.3 0.6 %copy.23 = bf16[64,512]{1,0:T(8,128)(2,1)} copy(bf16[64,512]{1,0:T(8,128)(2,1)S(1)} %copy-done.3) | data formatting | bytes 131072
  42.0 0.0 copy-done.2
  42.0 0.6 %copy.24 = f32[64,256]{1,0:T(8,128)} copy(f32[64,256]{1,0:T(8,128)S(1)} %copy-done.2) | data formatting | bytes 131072
  42.6 0.0 copy-done.1
  42.6 0.7 %copy.25 = f32[64,512]{1,0:T(8,128)} copy(f32[64,512]{1,0:T(8,128)S(1)} %copy-done.1) | data formatting | bytes 262144
Async XLA Ops:
  0.6 1.5 %copy-start.4 = (bf16[256,64]{0,1:T(8,128)(2,1)S(1)}, bf16[256,64]{0,1:T(8,128)(2,1)}, u32[]{:S(2)}) copy-start(bf16[256,64]{0,1:T(8,128)(2,1)} %param.13) | copy-start | bytes 98308
  38.8 1.7 %copy-start = (f32[256,64]{1,0:T(8,128)S(1)}, f32[256,64]{1,0:T(8,128)}, u32[]{:S(2)}) copy-start(f32[256,64]{1,0:T(8,128)} %get-tuple-element.7) | copy-start | bytes 196612
  40.5 0.8 %copy-start.3 = (bf16[64,512]{1,0:T(8,128)(2,1)S(1)}, bf16[64,512]{1,0:T(8,128)(2,1)}, u32[]{:S(2)}) copy-start(bf16[64,512]{1,0:T(8,128)(2,1)} %get-tuple-element.15) | copy-start | bytes 196612
  40.5 1.5 %copy-start.2 = (f32[64,256]{1,0:T(8,128)S(1)}, f32[64,256]{1,0:T(8,128)}, u32[]{:S(2)}) copy-start(f32[64,256]{1,0:T(8,128)} %get-tuple-element.18) | copy-start | bytes 196612
  41.3 1.3 %copy-start.1 = (f32[64,512]{1,0:T(8,128)S(1)}, f32[64,512]{1,0:T(8,128)}, u32[]{:S(2)}) copy-start(f32[64,512]{1,0:T(8,128)} %get-tuple-element.19) | copy-start | bytes 393220
where the time goes:
time: 43.5 us; the launch traced here: 43.3 us
  Pallas kernels  35.9 us (83%)
  local copies, waits for them, and re-layouts  6.65 us (15%)
  between operations  0.66 us (2%)
    pallas_call x1, Pallas kernels, on_device(): pl.pallas_call(functools.partial(body, groups, rings, scale), out_shape=(...  35.9 us
    unnamed x15, local copies, waits for them, and re-layouts  4.28 us
    pallas_call x2, local copies, waits for them, and re-layouts, on_device(): pl.pallas_call(functools.partial(body, groups, rings, scale), out_shape=(...  2.36 us

commit v1 on v0

v1 whole, which is shorter than its diff:
```python
import functools
import math

import jax
import jax.numpy as jnp
import numpy as np
from jax import lax
from jax.experimental import pallas as pl
from jax.experimental.pallas import tpu as pltpu
from jax.sharding import PartitionSpec as P

F32 = jnp.float32
BF16 = jnp.bfloat16
LANES = 128


def dft_tables(strides, lanes, chans):
    length = 2 * strides * lanes
    n1 = np.arange(strides)
    n2 = np.arange(lanes)
    half = np.arange(strides) + 0.5
    first = np.exp(-2j * np.pi * np.outer(half, n1) / (2 * strides))
    eye = np.eye(chans)
    first_re, first_im = np.kron(first.real, eye), np.kron(first.imag, eye)
    ahead = np.concatenate([first_re, first_im], 0)
    twist = np.repeat(np.exp(-2j * np.pi * np.outer(half, n2) / length), chans, axis=0)
    last = np.exp(-2j * np.pi * np.outer(n2, n2) / lanes)
    c, s = last.real, last.imag
    across = np.block([[c, s], [-s, c]])
    low = lambda a: jnp.asarray(a.astype(np.float32)).astype(BF16)
    wide = lambda a: jnp.asarray(a.astype(np.float32))
    return (
        low(ahead),
        low(ahead.T * (2.0 / length)),
        low(across),
        low(across.T),
        wide(np.stack([twist.real, twist.imag])),
    )


def each(count, step):
    if count <= 16:
        for k in range(count):
            step(k)
    else:
        lax.fori_loop(0, count, lambda k, carry: (step(k), carry)[1], 0)


def body(
    groups, rings,
    in_ref, wv_ref, wg_ref, wo_ref, filt_ref, grad_ref, ahead_hbm, back_hbm, across_hbm, return_hbm, twist_hbm,
    din_ref, dw_ref, dfil_ref,
    full_in, full_grad, got_filt, out_val, got_val, out_dif, got_dif,
    out_mix, got_mix, out_dv, got_dv, out_df, got_df,
    out_din, got_din, out_w, got_w, out_ws, got_ws, out_v, got_v, out_vs, got_vs,
    ahead_ref, back_ref, across_ref, return_ref, twist_ref,
    seq_send, seq_recv, ch_send, ch_recv, line_send, line_recv, table_sem,
):
    me = lax.axis_index("seq")
    mc = lax.axis_index("ch")
    ch_rows, tokens = in_ref.shape
    chans = ch_rows // groups
    tiles = tokens // LANES
    width = full_in.shape[0] * ch_rows
    barrier = pltpu.get_barrier_semaphore()

    def seq_peer(k):
        return lax.rem(me + k, groups)

    def ch_peer(k):
        return lax.rem(mc + k, rings)

    each(groups - 1, lambda k: pl.semaphore_signal(
        barrier, inc=1, device_id={"seq": seq_peer(k + 1)}, device_id_type=pl.DeviceIdType.MESH))
    each(rings - 1, lambda k: pl.semaphore_signal(
        barrier, inc=1, device_id={"ch": ch_peer(k + 1)}, device_id_type=pl.DeviceIdType.MESH))
    tables = [
        pltpu.make_async_copy(src, dst, table_sem.at[i])
        for i, (src, dst) in enumerate((
            (ahead_hbm, ahead_ref), (twist_hbm, twist_ref), (across_hbm, across_ref),
            (return_hbm, return_ref), (back_hbm, back_ref)))
    ]
    for table in tables:
        table.start()
    pl.semaphore_wait(barrier, groups + rings - 2)

    def seq_copy(stage, src, dst, k, pick):
        return pltpu.make_async_remote_copy(
            src_ref=src.at[seq_peer(k)] if pick else src,
            dst_ref=dst.at[me],
            send_sem=seq_send.at[stage, k],
            recv_sem=seq_recv.at[stage, k],
            device_id={"seq": seq_peer(k)},
            device_id_type=pl.DeviceIdType.MESH,
        )

    def ch_copy(src, dst, k):
        return pltpu.make_async_remote_copy(
            src_ref=src.at[ch_peer(k)],
            dst_ref=dst.at[mc],
            send_sem=ch_send.at[k],
            recv_sem=ch_recv.at[k],
            device_id={"ch": ch_peer(k)},
            device_id_type=pl.DeviceIdType.MESH,
        )

    def seq_start(stage, src, dst, pick=True):
        each(groups - 1, lambda k: seq_copy(stage, src, dst, k + 1, pick).start())

    def seq_wait(stage, src, dst, pick=True):
        each(groups - 1, lambda k: seq_copy(stage, src, dst, k + 1, pick).wait_recv())

    def seq_done(stage, src, dst, pick=True):
        each(groups - 1, lambda k: seq_copy(stage, src, dst, k + 1, pick).wait_send())

    wholes = (full_in, full_grad)
    owns = (in_ref, grad_ref)

    def hop(array, block, step, own):
        return pltpu.make_async_remote_copy(
            src_ref=owns[array] if own else wholes[array].at[block],
            dst_ref=wholes[array].at[block],
            send_sem=line_send.at[array, (step + 1) // 2, block],
            recv_sem=line_recv.at[array, block],
            device_id={"ch": mc + step},
            device_id_type=pl.DeviceIdType.MESH,
        )

    def can(step):
        return mc < rings - 1 if step == 1 else mc > 0

    def present(step, far):
        return mc >= far if step == 1 else mc < rings - far

    def line_open(array):
        for step in (1, -1):
            @pl.when(can(step))
            def _():
                hop(array, mc, step, True).start()

    def line_take(array, far):
        for step in (1, -1):
            @pl.when(present(step, far))
            def _():
                hop(array, mc - step * far, step, False).wait_recv()
                if far < rings - 1:
                    @pl.when(can(step))
                    def _():
                        hop(array, mc - step * far, step, False).start()

    def line_close(array):
        for step in (1, -1):
            @pl.when(can(step))
            def _():
                hop(array, mc, step, True).wait_send()
                for far in range(1, rings - 1):
                    @pl.when(present(step, far))
                    def _():
                        hop(array, mc - step * far, step, False).wait_send()

    line_open(0)
    line_open(1)
    seq_start(0, filt_ref, got_filt)
    full_in[mc] = in_ref[...]
    full_grad[mc] = grad_ref[...]
    got_filt[me] = filt_ref[me]

    def by_owner(x):
        x = x.reshape(groups, chans, tokens)
        return jnp.concatenate([x[:, :, j * LANES:(j + 1) * LANES] for j in range(tiles)], axis=1)

    def by_token(x):
        x = x.astype(F32)
        x = jnp.concatenate([x[:, j * chans:(j + 1) * chans, :] for j in range(tiles)], axis=2)
        return x.reshape(ch_rows, tokens)

    def stacked(ref):
        return jnp.concatenate([ref[p] for p in range(groups)], axis=0).astype(BF16)

    rows = ahead_ref.shape[1]

    def dot(a, b):
        return jnp.dot(a, b, preferred_element_type=F32)

    def spectrum(x):
        first = dot(ahead_ref[...], x)
        re, im = first[:rows], first[rows:]
        tw_re, tw_im = twist_ref[0], twist_ref[1]
        mid = jnp.concatenate([re * tw_re - im * tw_im, re * tw_im + im * tw_re], axis=1).astype(BF16)
        out = dot(mid, across_ref[...])
        return out[:, :LANES], out[:, LANES:]

    def signal(re, im):
        mid = dot(jnp.concatenate([re, im], axis=1).astype(BF16), return_ref[...])
        re, im = mid[:, :LANES], mid[:, LANES:]
        tw_re, tw_im = twist_ref[0], twist_ref[1]
        tall = jnp.concatenate([re * tw_re + im * tw_im, im * tw_re - re * tw_im], axis=0).astype(BF16)
        return dot(back_ref[...], tall).reshape(groups, tiles * chans, LANES)

    over_first = (((0,), (0,)), ((), ()))
    over_last = (((1,), (1,)), ((), ()))
    for far in range(1, rings - 1):
        line_take(0, far)
        line_take(1, far)

    for table in tables:
        table.wait()
    seq_wait(0, filt_ref, got_filt)
    by_tile = jnp.concatenate(
        [got_filt[p][:, j * LANES:(j + 1) * LANES] for p in range(groups) for j in range(tiles)], axis=0)
    f_re, f_im = spectrum(by_tile.astype(BF16))

    line_take(0, rings - 1)
    x_in = full_in[...].reshape(width, tokens)
    value = dot(wv_ref[...], x_in)
    out_val[...] = by_owner(value).astype(BF16)
    seq_start(1, out_val, got_val)
    got_val[me] = out_val[me]
    gate = dot(wg_ref[...], x_in)

    line_take(1, rings - 1)
    x_grad = full_grad[...].reshape(width, tokens)
    d_gated = dot(wo_ref[...], x_grad)
    out_dif[...] = by_owner(d_gated * gate).astype(BF16)
    seq_start(2, out_dif, got_dif)
    got_dif[me] = out_dif[me]

    seq_wait(1, out_val, got_val)
    v_re, v_im = spectrum(stacked(got_val))
    out_mix[...] = signal(f_re * v_re - f_im * v_im, f_re * v_im + f_im * v_re).astype(BF16)
    seq_start(3, out_mix, got_mix)
    got_mix[me] = out_mix[me]

    seq_wait(2, out_dif, got_dif)
    g_re, g_im = spectrum(stacked(got_dif))
    out_dv[...] = signal(f_re * g_re + f_im * g_im, f_re * g_im - f_im * g_re).astype(BF16)
    seq_start(4, out_dv, got_dv)
    got_dv[me] = out_dv[me]
    out_df[...] = signal(v_re * g_re + v_im * g_im, v_re * g_im - v_im * g_re).astype(BF16)
    seq_start(5, out_df, got_df)
    got_df[me] = out_df[me]

    parts = width // LANES

    def by_share(x):
        x = x.reshape(groups, chans, width)
        return jnp.concatenate([x[:, :, j * LANES:(j + 1) * LANES] for j in range(parts)], axis=1)

    def by_width(x):
        return jnp.concatenate([x[:, j * chans:(j + 1) * chans, :] for j in range(parts)], axis=2).reshape(ch_rows, width)

    def total(ref):
        out = ref[0].astype(F32)
        for p in range(1, ref.shape[0]):
            out = out + ref[p].astype(F32)
        return out.astype(BF16)

    seq_wait(3, out_mix, got_mix)
    mixed = by_token(got_mix[...])
    gated_out = (gate * mixed).astype(BF16)
    d_gate = (d_gated * mixed).astype(BF16)
    gate_term = lax.dot_general(d_gate, x_in, over_last, preferred_element_type=F32)
    out_term = lax.dot_general(gated_out, x_grad, over_last, preferred_element_type=F32)
    out_w[...] = jnp.concatenate([by_share(gate_term), by_share(out_term)], axis=1).astype(BF16)
    seq_start(6, out_w, got_w)
    got_w[me] = out_w[me]
    from_gate = lax.dot_general(wg_ref[...], d_gate, over_first, preferred_element_type=F32)

    seq_wait(4, out_dv, got_dv)
    d_value = by_token(got_dv[...]).astype(BF16)
    d_in = lax.dot_general(wv_ref[...], d_value, over_first, preferred_element_type=F32) + from_gate
    out_din[...] = d_in.reshape(rings, ch_rows, tokens).astype(BF16)
    each(rings - 1, lambda k: ch_copy(out_din, got_din, k + 1).start())
    value_term = lax.dot_general(d_value, x_in, over_last, preferred_element_type=F32)
    out_v[...] = by_share(value_term).astype(BF16)
    seq_start(8, out_v, got_v)
    got_v[me] = out_v[me]
    got_din[mc] = out_din[mc]

    seq_wait(6, out_w, got_w)
    out_ws[...] = total(got_w)
    seq_start(7, out_ws, got_ws, False)
    got_ws[me] = out_ws[...]

    seq_wait(5, out_df, got_df)
    dfil_ref[...] = by_token(got_df[...])

    seq_wait(8, out_v, got_v)
    out_vs[...] = total(got_v)
    seq_start(9, out_vs, got_vs, False)
    got_vs[me] = out_vs[...]

    seq_wait(7, out_ws, got_ws, False)
    half = parts * chans
    summed = got_ws[...].astype(F32)
    dw_ref[1] = by_width(summed[:, :half, :])
    dw_ref[2] = by_width(summed[:, half:, :])
    each(rings - 1, lambda k: ch_copy(out_din, got_din, k + 1).wait_recv())
    din_ref[...] = total(got_din)
    seq_wait(9, out_vs, got_vs, False)
    dw_ref[0] = by_width(got_vs[...].astype(F32))

    line_close(0)
    line_close(1)
    each(rings - 1, lambda k: ch_copy(out_din, got_din, k + 1).wait_send())
    for stage, src, dst, pick in (
        (0, filt_ref, got_filt, True), (1, out_val, got_val, True), (2, out_dif, got_dif, True),
        (3, out_mix, got_mix, True), (4, out_dv, got_dv, True), (5, out_df, got_df, True),
        (6, out_w, got_w, True), (7, out_ws, got_ws, False), (8, out_v, got_v, True), (9, out_vs, got_vs, False),
    ):
        seq_done(stage, src, dst, pick)


def finish(scale, din_ref, dw_ref, dfil_ref, din_out, dwv_out, dwg_out, dwo_out, dfil_out):
    din_out[...] = din_ref[...]
    dwv_out[...] = dw_ref[0] * scale
    dwg_out[...] = dw_ref[1] * scale
    dwo_out[...] = dw_ref[2] * scale
    dfil_out[...] = dfil_ref[...] * scale


def solution(mesh):
    groups, rings = mesh.shape["seq"], mesh.shape["ch"]

    def on_device(inputs, w_value, w_gate, w_out, filter_taps, grad_out):
        ch_rows, tokens = inputs.shape
        width = w_value.shape[0]
        chans, tiles, parts = ch_rows // groups, tokens // LANES, width // LANES
        tables = dft_tables(groups * tiles, LANES, chans)
        scale = 1.0 / math.sqrt(tokens * groups)
        vmem = pl.BlockSpec(memory_space=pltpu.VMEM)
        hbm = pl.BlockSpec(memory_space=pl.ANY)
        block = pltpu.VMEM((groups, tiles * chans, LANES), BF16)
        whole = pltpu.VMEM((rings, ch_rows, tokens), BF16)
        share = lambda count: [
            pltpu.VMEM((groups, count * parts * chans, LANES), BF16),
            pltpu.VMEM((groups, count * parts * chans, LANES), BF16),
            pltpu.VMEM((count * parts * chans, LANES), BF16),
            pltpu.VMEM((groups, count * parts * chans, LANES), BF16),
        ]
        tokens_out = jax.ShapeDtypeStruct((ch_rows, tokens), F32)
        weight_out = jax.ShapeDtypeStruct((ch_rows, width), F32)
        d_inputs, d_weights, d_filter = pl.pallas_call(
            functools.partial(body, groups, rings),
            out_shape=(
                jax.ShapeDtypeStruct((ch_rows, tokens), BF16),
                jax.ShapeDtypeStruct((3, ch_rows, width), F32),
                tokens_out,
            ),
            in_specs=[vmem] * 6 + [hbm] * 5,
            out_specs=(vmem,) * 3,
            scratch_shapes=[whole, whole, pltpu.VMEM((groups, chans, tokens), F32)] + [block] * 10
            + [whole, whole] + share(2) + share(1)
            + [pltpu.VMEM(table.shape, table.dtype) for table in tables] + [
                pltpu.SemaphoreType.DMA((10, groups)),
                pltpu.SemaphoreType.DMA((10, groups)),
                pltpu.SemaphoreType.DMA((rings,)),
                pltpu.SemaphoreType.DMA((rings,)),
                pltpu.SemaphoreType.DMA((2, 2, rings)),
                pltpu.SemaphoreType.DMA((2, rings)),
                pltpu.SemaphoreType.DMA((5,)),
            ],
            compiler_params=pltpu.CompilerParams(collective_id=0, has_side_effects=True),
        )(
            inputs, w_value.T, w_gate.T, w_out, filter_taps.reshape(groups, chans, tokens), grad_out, *tables,
        )
        d_inputs, d_w_value, d_w_gate, d_w_out, d_filter = pl.pallas_call(
            functools.partial(finish, scale),
            out_shape=(
                jax.ShapeDtypeStruct((ch_rows, tokens), BF16), weight_out, weight_out, weight_out, tokens_out,
            ),
            in_specs=[vmem] * 3,
            out_specs=(vmem,) * 5,
        )(d_inputs, d_weights, d_filter)
        return d_inputs, d_w_value.T, d_w_gate.T, d_w_out, d_filter

    return jax.shard_map(
        on_device,
        mesh=mesh,
        in_specs=(P("ch", "seq"), P(None, "ch"), P(None, "ch"), P("ch", None), P("ch", "seq"), P("ch", "seq")),
        out_specs=(P("ch", "seq"), P(None, "ch"), P(None, "ch"), P("ch", None), P("ch", "seq")),
        check_vma=False,
    )
```

time: 43.5 us -> 37.4 us (0.86)
  local copies, waits for them, and re-layouts: 6.65 us -> 0 us
  Pallas kernels: 35.9 us -> 36.6 us
    unnamed x15 -> x0, local copies, waits for them, and re-layouts: 4.28 us -> none
    pallas_call x2 -> x0, local copies, waits for them, and re-layouts: 2.36 us -> none  [on_device(): pl.pallas_call(functools.partial(body, groups, rings, scale), out_shape=(...]
    pallas_call x1 -> x2, Pallas kernels: 35.9 us -> 36.6 us  [the longest x1 34.8 us: on_device(): pl.pallas_call(functools.partial(body, groups, rings), out_shape=(jax.Sha...]
where the time goes in v1:
time: 37.4 us; the launch traced here: 37.2 us
  Pallas kernels  36.6 us (98%)
  between operations  0.64 us (2%)
    pallas_call x1, Pallas kernels, on_device(): pl.pallas_call(functools.partial(body, groups, rings), out_shape=(jax.Sha...  34.8 us
    pallas_call x1, Pallas kernels, on_device(): pl.pallas_call(functools.partial(finish, scale), out_shape=(jax.ShapeDtyp...  1.79 us

profile of v1, /device:TPU:0, one launch (start us, length us, event | category | flops | bytes accessed | tf_op | source)
XLA Modules:
  0.0 37.2 jit_solution(12201489034238882862)
XLA Ops:
  0.6 34.8 %shard_map.146 = (bf16[64,512]{1,0:T(8,128)(2,1)}, f32[3,64,256]{2,1,0:T(8,128)}, f32[64,512]{1,0:T(8,128)}) custom-call(bf16[64,512]{1,0:T(8,128)(2,1)} %in_ref.1, bf16[64,256]{1,0:T(8,128)(2,1)} %bitcast.6, bf16[64,256]{1,0:T(8,128)(2,1)} %bitcast.7, bf16[64,256]{1,0:T(8,128)(2,1)} %wo_ref.1, f32[8,8,512]{2,1,0:T(8,128)} %bitcast.5, ...), custom_call_target="tpu_custom_call" | custom-call | tf_op jit(solution)/shard_map/pallas_call | solution.py:343
  35.4 1.8 %shard_map.147 = (bf16[64,512]{1,0:T(8,128)(2,1)}, f32[64,256]{1,0:T(8,128)}, f32[64,256]{1,0:T(8,128)}, f32[64,256]{1,0:T(8,128)}, f32[64,512]{1,0:T(8,128)}) custom-call(bf16[64,512]{1,0:T(8,128)(2,1)} %get-tuple-element.13.din_ref, f32[3,64,256]{2,1,0:T(8,128)} %get-tuple-element.14.dw_ref, f32[64,512]{1,0:T(8,128)} %get-tuple-element.15.dfil_ref), custom_call_target="tpu_custom_call" | custom-call | tf_op jit(solution)/shard_map/pallas_call | solution.py:367
